TPU v7x, 256 devices: a whole 4x4x8 slice. The times are simulated.
256 devices in a mesh: gx: 8 (over z_hi, y), gy: 8 (over z_lo, core), gz: 4 (over x).
Axes of the slice: x: 4, y: 4, z: 8 (z_hi: 2, z_lo: 4; z = z_hi * 4 + z_lo), core: 2. Of those that a mesh axis runs over, the one named last changes fastest.
Arguments:
- concentration: float32 [128, 512, 512], P('gx', 'gy', 'gz'), may hold values from -6 to 6
- speed: float32 [3, 128, 512, 512], P(None, 'gx', 'gy', 'gz'), may hold values from 0.1 to 1
- signs: int32 [3, 128, 512, 512], P(None, 'gx', 'gy', 'gz'), may hold values from 0 to 1
- diffusivity: float32 [128, 512, 512], P('gx', 'gy', 'gz'), may hold values from 0.02 to 0.12
- shear: int32 [1], replicated, may hold values from 0 to 511
Outputs:
- final_field: float32 [128, 512, 512], P('gx', 'gy', 'gz')
All inputs are finite; a program needn't handle non-finite values.
Results may differ from a plain program's by a relative error of at most 0.00002.
Values sent between devices are 32-bit elements; how exact they have to be, the bound alone decides.
A program may use at most 64 MiB of HBM per device.

v0:
```python
import functools

import jax
import jax.numpy as jnp
from jax import lax
from jax.experimental import pallas as pl
from jax.experimental.pallas import tpu as pltpu
from jax.sharding import PartitionSpec as P

STEPS = 8
DT = 0.25
MESH = pl.DeviceIdType.MESH


def coefficients(diffusivity, velocities):
    base = DT * diffusivity
    sides = []
    for velocity in velocities:
        sides.append(base + DT * jnp.maximum(velocity, 0.0))
        sides.append(base + DT * jnp.minimum(velocity, 0.0))
    own = 1.0
    for side in sides:
        own = own - side
    return [own] + sides


def weigh(weights, cells):
    total = weights[0] * cells[0]
    for weight, cell in zip(weights[1:], cells[1:]):
        total = total + weight * cell
    return total


def kernel(q, sizes, r_ref, conc, speed, signs, diff, out, F, T, F1, T1, C, CT, CY, S, SPD, SGN, SB, LB, ST, XZS, XZR,
           YS, YR, YZR, ZS, ZR, CXR, CYS, CYR, CZS, CZR, load_sem, send_sem, recv_sem, csend_sem, crecv_sem, out_sem):
    nx, ny, nz = sizes
    X, Y, Z = 16, 64, 128
    tiles = Y // 8
    rounds = STEPS // 2
    gx, gy, gz = lax.axis_index("gx"), lax.axis_index("gy"), lax.axis_index("gz")
    lane = lax.broadcasted_iota(jnp.int32, (8, Z), 1)
    l0, l127, from_left = lane == 0, lane == Z - 1, (lane & 2) == 0
    lane16 = lax.broadcasted_iota(jnp.int32, (X, Z), 1)
    first16, last16, low16 = lane16 == 0, lane16 == Z - 1, lane16 < 64
    r = r_ref[0]
    slide = (gx == nx - 1, gx == 0)
    recv_slide = (gx == 0, gx == nx - 1)
    start = (jnp.where(recv_slide[0], r, 0), jnp.where(recv_slide[1], 64 - r, 64))

    def wrap(value, n):
        return lax.rem(value + 2 * n, n)

    def x_targets(d):
        sign = 1 if d == 0 else -1
        to = wrap(gx + sign, nx)
        shift = jnp.where(slide[d], q, 0) * sign
        return to, wrap(gy - shift, ny), wrap(gy - shift - sign, ny), wrap(gy - shift + sign, ny)

    zs = ((1, 0), (-1, 1))

    def x_messages(par):
        found = []
        for d in range(2):
            to, at_a, at_n, at_e = x_targets(d)
            yes, no = slide[d], jnp.logical_not(slide[d])
            ryes, rno = recv_slide[d], jnp.logical_not(recv_slide[d])
            planes = F.at[pl.ds(X, 2), pl.ds(8, Y)] if d == 0 else F.at[pl.ds(2, 2), pl.ds(8, Y)]
            near, near_slot = (X + 1, 1) if d == 0 else (2, 0)
            first, last = F.at[near, pl.ds(8, 8)], F.at[near, pl.ds(Y, 8)]
            a_row, n_row = (8, 72) if d == 0 else (72, 8)
            found.append((d, None, None, planes, SB.at[par, d, :, pl.ds(a_row, Y)], (to, at_a, gz)))
            found.append((2 + d, yes, ryes, planes, SB.at[par, d, :, pl.ds(n_row, Y)], (to, at_n, gz)))
            if d == 0:
                found.append((2 + d, no, rno, first, SB.at[par, d, near_slot, pl.ds(72, 8)], (to, at_n, gz)))
                found.append((4 + d, None, None, last, SB.at[par, d, near_slot, pl.ds(0, 8)], (to, at_e, gz)))
            else:
                found.append((2 + d, no, rno, last, SB.at[par, d, near_slot, pl.ds(64, 8)], (to, at_n, gz)))
                found.append((4 + d, None, None, first, SB.at[par, d, near_slot, pl.ds(136, 8)], (to, at_e, gz)))
            for step, slot in zs:
                side = wrap(gz + step, nz)
                found.append((6 + 2 * d + slot, None, None, XZS.at[d], XZR.at[par, d, 0, slot], (to, at_a, side)))
                found.append((10 + 2 * d + slot, yes, ryes, XZS.at[d], XZR.at[par, d, 1, slot], (to, at_n, side)))
        return found

    def yz_messages(par):
        found = []
        for d in range(2):
            to = wrap(gy + 1 - 2 * d, ny)
            found.append((14 + d, None, None, YS.at[d], YR.at[par, d], (gx, to, gz)))
            for step, slot in zs:
                found.append((18 + 2 * d + slot, None, None, YS.at[d, 0], YZR.at[par, d, slot],
                              (gx, to, wrap(gz + step, nz))))
        for step, slot in zs:
            found.append((16 + slot, None, None, ZS, ZR.at[par, slot], (gx, gy, wrap(gz + step, nz))))
        return found

    def cx_messages():
        found = []
        for d in range(2):
            to, at_a, at_n, _ = x_targets(d)
            a_row, n_row = (8, 72) if d == 0 else (72, 8)
            plane = S.at[:, X - 1] if d == 0 else S.at[:, 0]
            found.append((d, None, None, plane, CXR.at[d, :, pl.ds(a_row, Y)], (to, at_a, gz)))
            found.append((2 + d, slide[d], recv_slide[d], plane, CXR.at[d, :, pl.ds(n_row, Y)], (to, at_n, gz)))
        return found

    def cyz_messages():
        found = [(4 + d, None, None, CYS.at[d], CYR.at[d], (gx, wrap(gy + 1 - 2 * d, ny), gz)) for d in range(2)]
        for step, slot in zs:
            found.append((6 + slot, None, None, CZS, CZR.at[slot], (gx, gy, wrap(gz + step, nz))))
        return found

    def when(predicate, action):
        if predicate is None:
            action()
        else:
            pl.when(predicate)(action)

    def copy_of(message, sems):
        index, _, _, source, destination, device = message
        return pltpu.make_async_remote_copy(
            src_ref=source, dst_ref=destination, send_sem=sems[0].at[index],
            recv_sem=sems[1].at[index], device_id=device, device_id_type=MESH)

    def send(messages, sems):
        for message in messages:
            when(message[1], lambda m=message: copy_of(m, sems).start())

    def await_received(messages, sems):
        for message in messages:
            when(message[2], lambda m=message: copy_of(m, sems).wait_recv())

    def await_sent(messages, sems):
        for message in messages:
            when(message[1], lambda m=message: copy_of(m, sems).wait_send())

    def field_sems(par):
        return send_sem, recv_sem.at[par]

    coef_sems = (csend_sem, crecv_sem)

    loads = [
        pltpu.make_async_copy(conc, F.at[pl.ds(2, X), pl.ds(8, Y)], load_sem.at[0]),
        pltpu.make_async_copy(diff, S.at[0], load_sem.at[1]),
        pltpu.make_async_copy(speed, SPD, load_sem.at[2]),
        pltpu.make_async_copy(signs, SGN, load_sem.at[3]),
    ]
    for load in loads:
        load.start()
    barrier = pltpu.get_barrier_semaphore()
    for message in x_messages(0) + yz_messages(0):
        when(message[1], lambda m=message: pl.semaphore_signal(
            barrier, inc=1, device_id=m[5], device_id_type=MESH))
    sliding = jnp.logical_or(slide[0], slide[1])

    @pl.when(sliding)
    def _():
        pl.semaphore_wait(barrier, 20)

    @pl.when(jnp.logical_not(sliding))
    def _():
        pl.semaphore_wait(barrier, 18)

    def roll(value, amount):
        amount = amount % Z
        return value if amount == 0 else pltpu.roll(value, amount, 1)

    def pack_xz():
        for d, p in ((0, X + 1), (1, 2)):
            packed = roll(F[p, pl.ds(8, 8)], 2)
            for yt in range(1, tiles):
                packed = jnp.where((lane >> 2) == yt, roll(F[p, pl.ds(8 + 8 * yt, 8)], 4 * yt + 2), packed)
            XZS[d] = packed

    def pack_z(get, put):
        def some(h, _):
            packed = roll(get(4 * h, 0), 2)
            for i in range(1, 32):
                packed = jnp.where((lane >> 2) == i, roll(get(4 * h + i // 8, i % 8), 4 * i + 2), packed)
            put(h, packed)
            return 0

        lax.fori_loop(0, 4, some, 0)

    def put_zs(h, value):
        ZS[h] = value

    def pack_yz():
        for d, near, far in ((0, 71, 70), (1, 8, 9)):
            YS[d, 0] = F[pl.ds(2, X), near, :]
            YS[d, 1] = F[pl.ds(2, X), far, :]
        pack_z(lambda p, yt: F[2 + p, pl.ds(8 + 8 * yt, 8)], put_zs)

    loads[0].wait()
    pack_xz()
    send(x_messages(0), field_sems(0))
    pack_yz()
    send(yz_messages(0), field_sems(0))

    for load in loads[1:]:
        load.wait()

    def own_coefficients(p):
        for yt in range(tiles):
            rows = pl.ds(8 * yt, 8)
            velocities = []
            for axis in range(3):
                magnitude = SPD[axis, p, rows]
                velocity = jnp.where(SGN[axis, p, rows] > 0, magnitude, -magnitude)
                S[1 + axis, p, rows] = velocity
                velocities.append(velocity)
            for k, weight in enumerate(coefficients(S[0, p, rows], velocities)):
                C[k, 1 + p, rows] = weight

    def outer_coefficients(i, _):
        own_coefficients((X - 1) * i)
        return 0

    def inner_coefficients(p, _):
        own_coefficients(p)
        return 0

    lax.fori_loop(0, 2, outer_coefficients, 0)
    send(cx_messages(), coef_sems)
    lax.fori_loop(1, X - 1, inner_coefficients, 0)
    for d, row in ((0, Y - 1), (1, 0)):
        for a in range(4):
            CYS[d, a] = S[a, :, row, :]
    for a in range(4):
        def put_czs(h, value, a=a):
            CZS[a, h] = value

        pack_z(lambda p, yt, a=a: S[a, p, pl.ds(8 * yt, 8)], put_czs)
    send(cyz_messages(), coef_sems)
    await_received(cyz_messages(), coef_sems)
    for d in range(2):
        values = [CYR[d, a] for a in range(4)]
        for k, weight in enumerate(coefficients(values[0], values[1:])):
            CY[d, k] = weight

    def ghost_coefficients(h, _):
        merged = [jnp.where(from_left, CZR[0, a, h], CZR[1, a, h]) for a in range(4)]
        for i in range(32):
            values = [roll(m, -(4 * i + 2)) for m in merged]
            for k, weight in enumerate(coefficients(values[0], values[1:])):
                CT[k, 4 * h + i // 8, pl.ds(8 * (i % 8), 8)] = weight
        return 0

    lax.fori_loop(0, 4, ghost_coefficients, 0)

    def along_z(value, other):
        return roll(jnp.where(l127, other, value), 1), roll(jnp.where(l0, other, value), -1)

    def tile_of(field, weights, p, yt, value, below, above):
        rows = pl.ds(8 + 8 * yt, 8)
        return weigh(weights, (
            value, field[p - 1, rows], field[p + 1, rows], field[p, pl.ds(7 + 8 * yt, 8)],
            field[p, pl.ds(9 + 8 * yt, 8)], below, above))

    def plane(source, ghost, target, p):
        for yt in range(tiles):
            rows = pl.ds(8 + 8 * yt, 8)
            value = source[p, rows]
            below, above = along_z(value, ghost[p, rows])
            weights = [C[k, p - 1, pl.ds(8 * yt, 8)] for k in range(7)]
            target[p, rows] = tile_of(source, weights, p, yt, value, below, above)

    def ghost_plane(p):
        for yt in range(tiles):
            rows = pl.ds(8 + 8 * yt, 8)
            value = T[p, rows]
            below, above = along_z(value, F[p, rows])
            weights = [CT[k, p - 2, pl.ds(8 * yt, 8)] for k in range(7)]
            T1[p, rows] = tile_of(T, weights, p, yt, value, below, above)

    def first_inner(p, _):
        plane(F, T, F1, p)
        ghost_plane(p)
        return 0

    def first_outer(i, _):
        p = 2 + (X - 1) * i
        plane(F, T, F1, p)
        ghost_plane(p)
        return 0

    def first_beyond(i, _):
        plane(F, T, F1, 1 + (X + 1) * i)
        return 0

    def second_inner(p, _):
        plane(F1, T1, F, p)
        return 0

    def second_outer(i, _):
        plane(F1, T1, F, jnp.where(i < 2, 2 + i, X - 2 + i))
        return 0

    def step_pair(m, _):
        par = lax.rem(m, 2)
        sems = field_sems(par)
        await_received(yz_messages(par), sems)

        def unpack(h, _):
            merged = jnp.where(from_left, ZR[par, 0, h], ZR[par, 1, h])
            for i in range(32):
                T[2 + 4 * h + i // 8, pl.ds(8 + 8 * (i % 8), 8)] = roll(merged, -(4 * i + 2))
            return 0

        lax.fori_loop(0, 4, unpack, 0)
        for d, row in ((0, 7), (1, 72)):
            F[pl.ds(2, X), row, :] = YR[par, d, 0]
            T[pl.ds(2, X), row, :] = jnp.where(low16, YZR[par, d, 1], YZR[par, d, 0])
        lax.fori_loop(3, X + 1, first_inner, 0)

        await_received(x_messages(par), sems)
        for d in range(2):
            a_row, n_row = (8, 72) if d == 0 else (72, 8)
            for block, row in ((0, a_row), (1, n_row)):
                merged = jnp.where(from_left, XZR[par, d, block, 0], XZR[par, d, block, 1])
                for yt in range(tiles):
                    ST[d, pl.ds(row + 8 * yt, 8)] = roll(merged, -(4 * yt + 2))
            for i in range(2):
                LB[d, i] = SB[par, d, i]
            for i in range(2):
                F[(X + 2) * d + i] = LB[d, i, pl.ds(start[d], 80)]
            T[1 + (X + 1) * d, pl.ds(8, Y)] = ST[d, pl.ds(start[d] + 8, Y)]

        @pl.when(m == 0)
        def _():
            await_received(cx_messages(), coef_sems)
            for d in range(2):
                for yt in range(tiles):
                    values = [CXR[d, a, pl.ds(start[d] + 8 + 8 * yt, 8)] for a in range(4)]
                    for k, weight in enumerate(coefficients(values[0], values[1:])):
                        C[k, (X + 1) * d, pl.ds(8 * yt, 8)] = weight

        lax.fori_loop(0, 2, first_beyond, 0)
        lax.fori_loop(0, 2, first_outer, 0)
        for d, row in ((0, 7), (1, 72)):
            value = YR[par, d, 0]
            below = roll(jnp.where(last16, YZR[par, d, 0], value), 1)
            above = roll(jnp.where(first16, YZR[par, d, 1], value), -1)
            far, own = YR[par, d, 1], F[pl.ds(2, X), 8 if d == 0 else 71, :]
            y_low, y_high = (far, own) if d == 0 else (own, far)
            F1[pl.ds(2, X), row, :] = weigh([CY[d, k] for k in range(7)], (
                value, F[pl.ds(1, X), row, :], F[pl.ds(3, X), row, :], y_low, y_high, below, above))
        await_sent(x_messages(par) + yz_messages(par), sems)

        lax.fori_loop(0, 4, second_outer, 0)

        @pl.when(m < rounds - 1)
        def _():
            pack_xz()
            send(x_messages(1 - par), field_sems(1 - par))

        lax.fori_loop(4, X, second_inner, 0)

        @pl.when(m < rounds - 1)
        def _():
            pack_yz()
            send(yz_messages(1 - par), field_sems(1 - par))

        return 0

    lax.fori_loop(0, rounds, step_pair, 0)
    await_sent(cx_messages() + cyz_messages(), coef_sems)
    result = pltpu.make_async_copy(F.at[pl.ds(2, X), pl.ds(8, Y)], out, out_sem)
    result.start()
    result.wait()


def body(sizes, concentration, speed, signs, diffusivity, shear):
    X, Y, Z = concentration.shape
    f32, vmem, dma = jnp.float32, pltpu.VMEM, pltpu.SemaphoreType.DMA
    hbm = pl.BlockSpec(memory_space=pl.ANY)

    def call(q, r, *arrays):
        return pl.pallas_call(
            functools.partial(kernel, q, sizes),
            out_shape=jax.ShapeDtypeStruct((X, Y, Z), f32),
            in_specs=[pl.BlockSpec(memory_space=pltpu.SMEM)] + [hbm] * 4,
            out_specs=hbm,
            scratch_shapes=[
                vmem((X + 4, Y + 16, Z), f32),
                vmem((X + 4, Y + 16, Z), f32),
                vmem((X + 4, Y + 16, Z), f32),
                vmem((X + 4, Y + 16, Z), f32),
                vmem((7, X + 2, Y, Z), f32),
                vmem((7, X, Y, Z), f32),
                vmem((2, 7, X, Z), f32),
                vmem((4, X, Y, Z), f32),
                vmem((3, X, Y, Z), f32),
                vmem((3, X, Y, Z), jnp.int32),
                vmem((2, 2, 2, 144, Z), f32),
                vmem((2, 2, 144, Z), f32),
                vmem((2, 144, Z), f32),
                vmem((2, 8, Z), f32),
                vmem((2, 2, 2, 2, 8, Z), f32),
                vmem((2, 2, X, Z), f32),
                vmem((2, 2, 2, X, Z), f32),
                vmem((2, 2, 2, X, Z), f32),
                vmem((4, 8, Z), f32),
                vmem((2, 2, 4, 8, Z), f32),
                vmem((2, 4, 144, Z), f32),
                vmem((2, 4, X, Z), f32),
                vmem((2, 4, X, Z), f32),
                vmem((4, 4, 8, Z), f32),
                vmem((2, 4, 4, 8, Z), f32),
                dma((4,)), dma((22,)), dma((2, 22)), dma((8,)), dma((8,)), dma(()),
            ],
            compiler_params=pltpu.CompilerParams(
                collective_id=q, has_side_effects=True, vmem_limit_bytes=48 << 20),
        )(r, *arrays)

    offset = lax.rem(shear[0], sizes[1] * Y)
    branches = [functools.partial(call, q) for q in range(sizes[1])]
    return lax.switch(offset // Y, branches, (offset % Y)[None], concentration, speed, signs, diffusivity)


def solution(mesh):
    sizes = tuple(mesh.shape[name] for name in ("gx", "gy", "gz"))
    placed = (
        P("gx", "gy", "gz"),
        P(None, "gx", "gy", "gz"),
        P(None, "gx", "gy", "gz"),
        P("gx", "gy", "gz"),
        P(),
    )
    return jax.shard_map(
        functools.partial(body, sizes), mesh=mesh, in_specs=placed, out_specs=P("gx", "gy", "gz"), check_vma=False
    )
```

profile of v0, /device:TPU:33, one launch (start us, length us, event | category | flops | bytes accessed | tf_op | source)
XLA Modules:
  0.0 76.9 jit_solution(5073087953880589118)
XLA Ops:
  0.7 75.4 %conditional.1 = (f32[16,64,128]{2,1,0:T(8,128)S(1)}) conditional(s32[]{:T(128)} %clamp.3, (s32[]{:T(128)}, f32[16,64,128]{2,1,0:T(8,128)}, f32[3,16,64,128]{3,2,1,0:T(8,128)}, s32[3,16,64,128]{3,2,1,0:T(8,128)}, f32[16,64,128]{2,1,0:T(8,128)}, /*index=5*/s32[]{:T(128)}, s32[]{:T(128)}, pred[]{:T(512)}, ...), branch_computations={%region_0.1_spmd.clone, %region_1.2_spmd.clone, %region_2.3_spmd.c... | conditional | flops 4 | bytes 45 | solution.py:418
  0.9 74.9 %branch_7_fun.1 = f32[16,64,128]{2,1,0:T(8,128)S(1)} custom-call(s32[1]{0:T(128)} %bitcast.8.r_ref, f32[16,64,128]{2,1,0:T(8,128)} %get-tuple-element.406.conc, f32[3,16,64,128]{3,2,1,0:T(8,128)} %get-tuple-element.407.speed, s32[3,16,64,128]{3,2,1,0:T(8,128)} %get-tuple-element.408.signs, f32[16,64,128]{2,1,0:T(8,128)} %get-tuple-element.409.diff), custom_call_target="tpu_custom_call" | custom-call | tf_op jit(solution)/shard_map/cond/branch_7_fun/pallas_call | solution.py:379
  76.1 0.8 %copy.96 = f32[16,64,128]{2,1,0:T(8,128)} copy(f32[16,64,128]{2,1,0:T(8,128)S(1)} %get-tuple-element.134) | data formatting | bytes 1048576
where the time goes:
time: 77 us; the launch traced here: 76.9 us
  Pallas kernels  74.9 us (97%)
  local copies, waits for them, and re-layouts  0.8 us (1%)
    pallas_call x1, Pallas kernels, call(): pl.pallas_call(functools.partial(kernel, q, sizes), out_shape=jax.ShapeDt...  74.9 us

commit v1 on v0

--- a/solution.py
+++ b/solution.py
@@ -97,11 +97,17 @@
     def cx_messages():
         found = []
         for d in range(2):
-            to, at_a, at_n, _ = x_targets(d)
+            to, at_a, _, _ = x_targets(d)
+            plane = S.at[:, pl.ds(Y * (X - 1), Y)] if d == 0 else S.at[:, pl.ds(0, Y)]
+            found.append((d, None, None, plane, CXR.at[d, :, pl.ds(8 if d == 0 else 72, Y)], (to, at_a, gz)))
+        return found
+
+    def cx_forwards():
+        found = []
+        for d in range(2):
             a_row, n_row = (8, 72) if d == 0 else (72, 8)
-            plane = S.at[:, X - 1] if d == 0 else S.at[:, 0]
-            found.append((d, None, None, plane, CXR.at[d, :, pl.ds(a_row, Y)], (to, at_a, gz)))
-            found.append((2 + d, slide[d], recv_slide[d], plane, CXR.at[d, :, pl.ds(n_row, Y)], (to, at_n, gz)))
+            found.append((2 + d, recv_slide[d], recv_slide[d], CXR.at[d, :, pl.ds(a_row, Y)],
+                          CXR.at[d, :, pl.ds(n_row, Y)], (gx, wrap(gy - 1 + 2 * d, ny), gz)))
         return found
 
     def cyz_messages():
@@ -141,9 +147,9 @@
 
     loads = [
         pltpu.make_async_copy(conc, F.at[pl.ds(2, X), pl.ds(8, Y)], load_sem.at[0]),
-        pltpu.make_async_copy(diff, S.at[0], load_sem.at[1]),
-        pltpu.make_async_copy(speed, SPD, load_sem.at[2]),
-        pltpu.make_async_copy(signs, SGN, load_sem.at[3]),
+        pltpu.make_async_copy(diff, S.at[0, pl.ds(0, X * Y)], load_sem.at[1]),
+        pltpu.make_async_copy(speed, SPD.at[:, pl.ds(0, X * Y)], load_sem.at[2]),
+        pltpu.make_async_copy(signs, SGN.at[:, pl.ds(0, X * Y)], load_sem.at[3]),
     ]
     for load in loads:
         load.start()
@@ -151,15 +157,6 @@
     for message in x_messages(0) + yz_messages(0):
         when(message[1], lambda m=message: pl.semaphore_signal(
             barrier, inc=1, device_id=m[5], device_id_type=MESH))
-    sliding = jnp.logical_or(slide[0], slide[1])
-
-    @pl.when(sliding)
-    def _():
-        pl.semaphore_wait(barrier, 20)
-
-    @pl.when(jnp.logical_not(sliding))
-    def _():
-        pl.semaphore_wait(barrier, 18)
 
     def roll(value, amount):
         amount = amount % Z
@@ -180,7 +177,8 @@
             put(h, packed)
             return 0
 
-        lax.fori_loop(0, 4, some, 0)
+        for h in range(4):
+            some(h, 0)
 
     def put_zs(h, value):
         ZS[h] = value
@@ -193,45 +191,52 @@
 
     loads[0].wait()
     pack_xz()
-    send(x_messages(0), field_sems(0))
     pack_yz()
-    send(yz_messages(0), field_sems(0))
-
     for load in loads[1:]:
         load.wait()
 
     def own_coefficients(p):
         for yt in range(tiles):
-            rows = pl.ds(8 * yt, 8)
+            rows = pl.ds(pl.multiple_of(Y * p + 8 * yt, 8), 8)
             velocities = []
             for axis in range(3):
-                magnitude = SPD[axis, p, rows]
-                velocity = jnp.where(SGN[axis, p, rows] > 0, magnitude, -magnitude)
-                S[1 + axis, p, rows] = velocity
+                magnitude = SPD[axis, rows]
+                velocity = jnp.where(SGN[axis, rows] > 0, magnitude, -magnitude)
+                S[1 + axis, rows] = velocity
                 velocities.append(velocity)
-            for k, weight in enumerate(coefficients(S[0, p, rows], velocities)):
-                C[k, 1 + p, rows] = weight
-
-    def outer_coefficients(i, _):
-        own_coefficients((X - 1) * i)
-        return 0
-
-    def inner_coefficients(p, _):
+            for k, weight in enumerate(coefficients(S[0, rows], velocities)):
+                C[tiles * (1 + p) + yt, k] = weight
+
+    def each_coefficients(p, _):
         own_coefficients(p)
         return 0
 
-    lax.fori_loop(0, 2, outer_coefficients, 0)
-    send(cx_messages(), coef_sems)
-    lax.fori_loop(1, X - 1, inner_coefficients, 0)
+    lax.fori_loop(0, X, each_coefficients, 0)
     for d, row in ((0, Y - 1), (1, 0)):
         for a in range(4):
-            CYS[d, a] = S[a, :, row, :]
-    for a in range(4):
-        def put_czs(h, value, a=a):
+            CYS[d, a] = S[a, pl.ds(row, X, stride=Y), :]
+    def pack_coefficients(a, _):
+        def put_czs(h, value):
             CZS[a, h] = value
 
-        pack_z(lambda p, yt, a=a: S[a, p, pl.ds(8 * yt, 8)], put_czs)
+        pack_z(lambda p, yt: S[a, pl.ds(Y * p + 8 * yt, 8)], put_czs)
+        return 0
+
+    lax.fori_loop(0, 4, pack_coefficients, 0)
+    sliding = jnp.logical_or(slide[0], slide[1])
+
+    @pl.when(sliding)
+    def _():
+        pl.semaphore_wait(barrier, 20)
+
+    @pl.when(jnp.logical_not(sliding))
+    def _():
+        pl.semaphore_wait(barrier, 18)
+
+    send(x_messages(0), field_sems(0))
+    send(yz_messages(0), field_sems(0))
     send(cyz_messages(), coef_sems)
+    send(cx_messages(), coef_sems)
     await_received(cyz_messages(), coef_sems)
     for d in range(2):
         values = [CYR[d, a] for a in range(4)]
@@ -243,7 +248,7 @@
         for i in range(32):
             values = [roll(m, -(4 * i + 2)) for m in merged]
             for k, weight in enumerate(coefficients(values[0], values[1:])):
-                CT[k, 4 * h + i // 8, pl.ds(8 * (i % 8), 8)] = weight
+                CT[32 * h + i, k] = weight
         return 0
 
     lax.fori_loop(0, 4, ghost_coefficients, 0)
@@ -262,7 +267,7 @@
             rows = pl.ds(8 + 8 * yt, 8)
             value = source[p, rows]
             below, above = along_z(value, ghost[p, rows])
-            weights = [C[k, p - 1, pl.ds(8 * yt, 8)] for k in range(7)]
+            weights = [C[tiles * (p - 1) + yt, k] for k in range(7)]
             target[p, rows] = tile_of(source, weights, p, yt, value, below, above)
 
     def ghost_plane(p):
@@ -270,30 +275,18 @@
             rows = pl.ds(8 + 8 * yt, 8)
             value = T[p, rows]
             below, above = along_z(value, F[p, rows])
-            weights = [CT[k, p - 2, pl.ds(8 * yt, 8)] for k in range(7)]
+            weights = [CT[tiles * (p - 2) + yt, k] for k in range(7)]
             T1[p, rows] = tile_of(T, weights, p, yt, value, below, above)
 
-    def first_inner(p, _):
-        plane(F, T, F1, p)
-        ghost_plane(p)
-        return 0
-
-    def first_outer(i, _):
-        p = 2 + (X - 1) * i
-        plane(F, T, F1, p)
-        ghost_plane(p)
-        return 0
-
-    def first_beyond(i, _):
-        plane(F, T, F1, 1 + (X + 1) * i)
-        return 0
-
-    def second_inner(p, _):
-        plane(F1, T1, F, p)
-        return 0
-
-    def second_outer(i, _):
-        plane(F1, T1, F, jnp.where(i < 2, 2 + i, X - 2 + i))
+    def first_inner(i, _):
+        for p in (3 + 2 * i, 4 + 2 * i):
+            plane(F, T, F1, p)
+            ghost_plane(p)
+        return 0
+
+    def second_inner(i, _):
+        for p in range(4):
+            plane(F1, T1, F, 4 + 4 * i + p)
         return 0
 
     def step_pair(m, _):
@@ -307,11 +300,17 @@
                 T[2 + 4 * h + i // 8, pl.ds(8 + 8 * (i % 8), 8)] = roll(merged, -(4 * i + 2))
             return 0
 
-        lax.fori_loop(0, 4, unpack, 0)
+        for h in range(4):
+            unpack(h, 0)
         for d, row in ((0, 7), (1, 72)):
             F[pl.ds(2, X), row, :] = YR[par, d, 0]
             T[pl.ds(2, X), row, :] = jnp.where(low16, YZR[par, d, 1], YZR[par, d, 0])
-        lax.fori_loop(3, X + 1, first_inner, 0)
+        lax.fori_loop(0, X // 2 - 1, first_inner, 0)
+
+        @pl.when(m == 0)
+        def _():
+            await_received(cx_messages(), coef_sems)
+            send(cx_forwards(), coef_sems)
 
         await_received(x_messages(par), sems)
         for d in range(2):
@@ -323,20 +322,22 @@
             for i in range(2):
                 LB[d, i] = SB[par, d, i]
             for i in range(2):
-                F[(X + 2) * d + i] = LB[d, i, pl.ds(start[d], 80)]
+                F[(X + 2) * d + i, pl.ds(0, 80)] = LB[d, i, pl.ds(start[d], 80)]
             T[1 + (X + 1) * d, pl.ds(8, Y)] = ST[d, pl.ds(start[d] + 8, Y)]
 
         @pl.when(m == 0)
         def _():
-            await_received(cx_messages(), coef_sems)
+            await_received(cx_forwards(), coef_sems)
             for d in range(2):
                 for yt in range(tiles):
                     values = [CXR[d, a, pl.ds(start[d] + 8 + 8 * yt, 8)] for a in range(4)]
                     for k, weight in enumerate(coefficients(values[0], values[1:])):
-                        C[k, (X + 1) * d, pl.ds(8 * yt, 8)] = weight
-
-        lax.fori_loop(0, 2, first_beyond, 0)
-        lax.fori_loop(0, 2, first_outer, 0)
+                        C[tiles * (X + 1) * d + yt, k] = weight
+
+        for p in (1, X + 2, 2, X + 1):
+            plane(F, T, F1, p)
+        for p in (2, X + 1):
+            ghost_plane(p)
         for d, row in ((0, 7), (1, 72)):
             value = YR[par, d, 0]
             below = roll(jnp.where(last16, YZR[par, d, 0], value), 1)
@@ -347,14 +348,15 @@
                 value, F[pl.ds(1, X), row, :], F[pl.ds(3, X), row, :], y_low, y_high, below, above))
         await_sent(x_messages(par) + yz_messages(par), sems)
 
-        lax.fori_loop(0, 4, second_outer, 0)
+        for p in (2, 3, X, X + 1):
+            plane(F1, T1, F, p)
 
         @pl.when(m < rounds - 1)
         def _():
             pack_xz()
             send(x_messages(1 - par), field_sems(1 - par))
 
-        lax.fori_loop(4, X, second_inner, 0)
+        lax.fori_loop(0, X // 4 - 1, second_inner, 0)
 
         @pl.when(m < rounds - 1)
         def _():
@@ -364,7 +366,7 @@
         return 0
 
     lax.fori_loop(0, rounds, step_pair, 0)
-    await_sent(cx_messages() + cyz_messages(), coef_sems)
+    await_sent(cx_messages() + cx_forwards() + cyz_messages(), coef_sems)
     result = pltpu.make_async_copy(F.at[pl.ds(2, X), pl.ds(8, Y)], out, out_sem)
     result.start()
     result.wait()
@@ -382,16 +384,16 @@
             in_specs=[pl.BlockSpec(memory_space=pltpu.SMEM)] + [hbm] * 4,
             out_specs=hbm,
             scratch_shapes=[
-                vmem((X + 4, Y + 16, Z), f32),
-                vmem((X + 4, Y + 16, Z), f32),
-                vmem((X + 4, Y + 16, Z), f32),
-                vmem((X + 4, Y + 16, Z), f32),
-                vmem((7, X + 2, Y, Z), f32),
-                vmem((7, X, Y, Z), f32),
+                vmem((X + 4, Y + 24, Z), f32),
+                vmem((X + 4, Y + 24, Z), f32),
+                vmem((X + 4, Y + 24, Z), f32),
+                vmem((X + 4, Y + 24, Z), f32),
+                vmem(((X + 2) * Y // 8, 7, 8, Z), f32),
+                vmem((X * Y // 8, 7, 8, Z), f32),
                 vmem((2, 7, X, Z), f32),
-                vmem((4, X, Y, Z), f32),
-                vmem((3, X, Y, Z), f32),
-                vmem((3, X, Y, Z), jnp.int32),
+                vmem((4, X * Y + 8, Z), f32),
+                vmem((3, X * Y + 8, Z), f32),
+                vmem((3, X * Y + 8, Z), jnp.int32),
                 vmem((2, 2, 2, 144, Z), f32),
                 vmem((2, 2, 144, Z), f32),
                 vmem((2, 144, Z), f32),
@@ -415,7 +417,8 @@
 
     offset = lax.rem(shear[0], sizes[1] * Y)
     branches = [functools.partial(call, q) for q in range(sizes[1])]
-    return lax.switch(offset // Y, branches, (offset % Y)[None], concentration, speed, signs, diffusivity)
+    return lax.switch(offset // Y, branches, (offset % Y)[None], concentration,
+                      speed.reshape(3, X * Y, Z), signs.reshape(3, X * Y, Z), diffusivity.reshape(X * Y, Z))
 
 
 def solution(mesh):

time: 77 us -> 71 us (0.922)
  the two profiles are of different devices: /device:TPU:33 before, /device:TPU:1 now
where the time goes in v1:
time: 71 us; the launch traced here: 69.8 us
  Pallas kernels  68 us (96%)
  local copies, waits for them, and re-layouts  0.8 us (1%)
    pallas_call x1, Pallas kernels, call(): pl.pallas_call(functools.partial(kernel, q, sizes), out_shape=jax.ShapeDt...  68 us

profile of v1, /device:TPU:1, one launch (start us, length us, event | category | flops | bytes accessed | tf_op | source)
XLA Modules:
  0.0 69.8 jit_solution(7529812149253748603)
XLA Ops:
  0.7 68.3 %conditional.1 = (f32[16,64,128]{2,1,0:T(8,128)S(1)}) conditional(s32[]{:T(128)} %clamp.3, (s32[]{:T(128)}, f32[16,64,128]{2,1,0:T(8,128)}, f32[3,16,64,128]{3,2,1,0:T(8,128)}, s32[3,16,64,128]{3,2,1,0:T(8,128)}, f32[16,64,128]{2,1,0:T(8,128)}, /*index=5*/s32[]{:T(128)}, s32[]{:T(128)}, pred[]{:T(512)}, ...), branch_computations={%region_0.1_spmd.clone, %region_1.2_spmd.clone, %region_2.3_spmd.c... | conditional | flops 4 | bytes 45 | solution.py:420
  0.7 68.0 %branch_1_fun.1 = f32[16,64,128]{2,1,0:T(8,128)S(1)} custom-call(s32[1]{0:T(128)} %bitcast.5.r_ref, f32[16,64,128]{2,1,0:T(8,128)} %get-tuple-element.322.conc, f32[3,1024,128]{2,1,0:T(8,128)} %bitcast.37, s32[3,1024,128]{2,1,0:T(8,128)} %bitcast.45, f32[1024,128]{1,0:T(8,128)} %bitcast.53), custom_call_target="tpu_custom_call" | custom-call | tf_op jit(solution)/shard_map/cond/branch_1_fun/pallas_call | solution.py:381
  69.0 0.8 %copy.96 = f32[16,64,128]{2,1,0:T(8,128)} copy(f32[16,64,128]{2,1,0:T(8,128)S(1)} %get-tuple-element.134) | data formatting | bytes 1048576
